TPU v7x, 32 devices: a whole 2x2x4 slice. The times are simulated.
32 devices in a mesh: tm: 2 (over x), src: 16 (over z, y, core).
Axes of the slice: x: 2, y: 2, z: 4, core: 2. Of those that a mesh axis runs over, the one named last changes fastest.
Arguments:
- design: float32 [16, 524288], P(None, ('tm', 'src')), may hold values from -2 to 2
- unit_index: int32 [524288], P(('tm', 'src')), may hold values from 0 to 255, as said below
- residual: float32 [524288], P(('tm', 'src')), may hold values from -6 to 6
- weight: float32 [524288], P(('tm', 'src')), may hold values from 0.25 to 4
- obs_count: int32 [32], P(('tm', 'src')), may hold values from 1 to 16384, as said below
- damping: float32 [256], P(('tm', 'src')), may hold values from 1 to 10
Outputs:
- solution: float32 [16, 256], P(None, ('tm', 'src'))
- misfit: float32 [], replicated
Inputs may be any that keep to these rules, and one draw needn't show every extreme that they name: `unit_index`: an observation on a device of tm index g names a unit in [g * 128, (g + 1) * 128). `obs_count`: some device has all 16384 slots live.
All inputs are finite; a program needn't handle non-finite values.
Results may differ from a plain program's by a relative error of at most 0.0003.
Values sent between devices are 32-bit elements; how exact they have to be, the bound alone decides.
No kernel may reach another device: no remote copies, remote signals or barrier semaphores. Data moves between devices by JAX's collectives and lax.ppermute only.
A program may use at most 64 MiB of HBM per device.

v0:
```python
import jax
import jax.numpy as jnp
from jax import lax
from jax.sharding import PartitionSpec as P


def make_reader(stacked):

    def reader(row, column):
        return stacked[row * 16 + column]

    return reader


def block_solve(reader, rhs, damping):
    lower = {}
    for j in range(16):
        running = reader(j, j) + damping
        for k in range(j):
            running = running - lower[j, k] * lower[j, k]
        diag_term = jnp.sqrt(running)
        lower[j, j] = diag_term
        for i in range(j + 1, 16):
            running = reader(i, j)
            for k in range(j):
                running = running - lower[i, k] * lower[j, k]
            lower[i, j] = running / diag_term
    forward = []
    for i in range(16):
        running = rhs[i]
        for k in range(i):
            running = running - lower[i, k] * forward[k]
        forward.append(running / lower[i, i])
    backward = [None] * 16
    for i in range(15, -1, -1):
        running = forward[i]
        for k in range(i + 1, 16):
            running = running - lower[k, i] * backward[k]
        backward[i] = running / lower[i, i]
    return jnp.stack(backward)


def quadratic_terms(reader, rhs, solution_own):
    quadratic = jnp.zeros((), jnp.float32)
    for i in range(16):
        applied = jnp.zeros_like(solution_own[0])
        for j in range(16):
            applied = applied + reader(max(i, j), min(i, j)) * solution_own[j]
        quadratic = quadratic + jnp.sum(solution_own[i] * applied)
    return quadratic - 2.0 * jnp.sum(solution_own * rhs)


def on_device(design, unit_index, residual, weight, obs_count, damping):
    n_source = lax.axis_size("src")
    own_units = damping.shape[0]
    units_group = own_units * n_source
    slots = design.shape[1]
    local_unit = unit_index - lax.axis_index("tm") * units_group
    weights_on = jnp.where(
        jnp.arange(slots, dtype=jnp.int32) < obs_count[0], weight, jnp.zeros_like(weight)
    )
    block_rows = 1024
    turns = slots // block_rows
    pair_count = 256

    def pair_rows(rows):
        return (rows[:, None, :] * rows[None, :, :]).reshape(256, rows.shape[1])

    unit_range = jnp.arange(units_group, dtype=jnp.int32)

    def accumulate(step, partial_value):
        begin = step * block_rows
        rows = lax.dynamic_slice_in_dim(design, begin, block_rows, 1)
        units_of = lax.dynamic_slice_in_dim(local_unit, begin, block_rows, 0)
        resid = lax.dynamic_slice_in_dim(residual, begin, block_rows, 0)
        weights_blk = lax.dynamic_slice_in_dim(weights_on, begin, block_rows, 0)
        stacked = jnp.concatenate(
            [pair_rows(rows) * weights_blk, rows * (weights_blk * resid)], axis=0
        )
        one_hot = (units_of[:, None] == unit_range[None, :]).astype(jnp.float32)
        return partial_value + jnp.dot(
            stacked, one_hot, precision=lax.Precision.HIGHEST, preferred_element_type=jnp.float32
        )

    start = jnp.zeros((pair_count + 16, units_group), jnp.float32)
    partial_value = lax.fori_loop(0, turns, accumulate, start)
    own_part = lax.psum_scatter(partial_value, "src", scatter_dimension=1, tiled=True)
    solution_own = block_solve(make_reader(own_part), own_part[pair_count:], damping)
    unit_terms = quadratic_terms(make_reader(own_part), own_part[pair_count:], solution_own)
    before = jnp.sum(weights_on * residual * residual)
    chi_total, weight_total = lax.psum((before + unit_terms, jnp.sum(weights_on)), ("tm", "src"))
    return (solution_own, chi_total / weight_total)


def solution(mesh):
    placed = (
        P(None, ("tm", "src")),
        P(("tm", "src")),
        P(("tm", "src")),
        P(("tm", "src")),
        P(("tm", "src")),
        P(("tm", "src")),
    )
    return jax.shard_map(
        on_device,
        mesh=mesh,
        in_specs=placed,
        out_specs=(P(None, ("tm", "src")), P()),
        check_vma=False,
    )
```

profile of v0, /device:TPU:0, one launch (start us, length us, event | category | flops | bytes accessed | tf_op | source)
XLA Modules:
  0.0 241.2 jit_solution(16647316104159535777)
XLA Ops:
  8.7 1.6 fusion.56
  10.3 42.7 %while.14 = (s32[]{:T(128)}, f32[272,128]{1,0:T(8,128)S(1)}, f32[16,16384]{1,0:T(8,128)}, f32[16384]{0:T(1024)S(1)}, f32[16384]{0:T(1024)}, /*index=5*/s32[16384...) while((s32[]{:T(128)}, f32[272,128]{1,0:T(8,128)S(1)}, f32[16,16384]{1,0:T(8,128)}, ...), condition=%wide.region_1.2_spmd.clone, body=%wide.region_0.1_spmd.clone.sunk | while | flops 428839936 | bytes 4837545 | solution.py:86
  11.0 0.8 broadcast_multiply_fusion.4
  13.7 0.8 broadcast_multiply_fusion.4
  16.3 0.8 broadcast_multiply_fusion.4
  19.0 0.8 broadcast_multiply_fusion.4
  24.4 0.8 broadcast_multiply_fusion.4
  27.0 0.8 broadcast_multiply_fusion.4
  29.7 0.8 broadcast_multiply_fusion.4
  54.9 90.6 %all-reduce.4.cloned.1.call-done = f32[272,128]{1,0:T(8,128)} async-done(((f32[272,128]{1,0:T(8,128)}), f32[272,128]{1,0:T(8,128)}) %all-reduce.4.cloned.1.call-update) | async-done | bytes 139280
  145.5 1.0 subtract_divide_fusion.110
  146.4 1.2 subtract_sqrt_fusion.8
  147.7 2.8 %subtract_divide_fusion.29 = (f32[8]{0:T(128)S(1)}, f32[8]{0:T(128)S(1)}, f32[8]{0:T(128)S(1)}, f32[8]{0:T(128)S(1)}, f32[8]{0:T(128)S(1)}, /*index=5*/f32[8]{0:...) fusion(f32[272,128]{1,0:T(8,128)} %all-reduce.4.cloned.1.call-d, ...), kind=kLoop, calls=%fused_computation.264 | loop fusion | flops 10472 | bytes 10624 | tf_op jit(solution)/shard_map/div | solution.py:33
  150.5 1.5 subtract_divide_fusion.15
  152.0 1.9 multiply_reduce_fusion
  154.6 1.4 fusion.9
  156.8 1.5 multiply_reduce_fusion.14
  158.2 1.4 multiply_reduce_fusion.15
  161.0 1.5 multiply_reduce_fusion.13
  163.2 1.5 multiply_reduce_fusion.12
  165.3 1.5 multiply_reduce_fusion.11
  167.5 1.5 multiply_reduce_fusion.10
  169.7 1.5 multiply_reduce_fusion.9
  171.8 1.5 multiply_reduce_fusion.8
  174.0 1.5 multiply_reduce_fusion.7
  176.2 1.5 multiply_reduce_fusion.6
  178.3 1.5 multiply_reduce_fusion.5
  180.5 1.5 multiply_reduce_fusion.4
  182.7 1.5 multiply_reduce_fusion.3
  184.8 1.5 multiply_reduce_fusion.2
  187.0 1.5 multiply_reduce_fusion.1
  190.5 41.3 %all-reduce.1 = (f32[]{:T(128)}, f32[]{:T(128)}) all-reduce(f32[]{:T(128)S(6)} %add.1126, f32[]{:T(128)} %get-tuple-element.154), channel_id=1, replica_groups=mesh['tm'=2,'src'=16] {'tm','src'}, use_global_device_ids=true, to_apply=%region_21.22 | all-reduce | flops 2 | bytes 16 | tf_op jit(solution)/shard_map/psum | solution.py:91
  (102 shorter events, 38.7 us)
Async XLA Ops:
  7.2 138.3 %all-reduce.4.cloned.1.call-start = ((), (), s32[]{:S(2)}) async-start(), calls=%async_computation | async-start | bytes 278528
  10.3 43.4 %copy-start.2 = (u32[32]{0:T(128)S(1)}, u32[32]{0:T(128)}, u32[]{:S(2)}) copy-start(u32[32]{0:T(128)} %constant.48) | copy-start | bytes 388
  10.3 135.2 %copy-start.1 = (f32[8]{0:T(128)S(1)}, f32[8]{0:T(128)}, u32[]{:S(2)}) copy-start(f32[8]{0:T(128)} %param.13) | copy-start | bytes 100
  53.0 0.7 copy-start
Sparse Core Ops, SparseCore 0:
  53.8 91.6 all-reduce.3
where the time goes:
time: 244 us; the launch traced here: 241 us
  waiting for transfers between devices  90.6 us (37%)
  other arithmetic  62.9 us (26%)
  blocking collectives  41.3 us (17%)
  between operations  30.2 us (12%)
  matrix products  13.1 us (5%)
    unnamed x2, waiting for transfers between devices  90.6 us
    psum x1, blocking collectives, on_device(): lax.psum((before + unit_terms, jnp.sum(weights_on)), ('tm', 'src'))  41.3 us
    reduce_sum x16, other arithmetic, quadratic_terms(): quadratic = quadratic + jnp.sum(solution_own[i] * applied)  24 us
    mul x16, other arithmetic, accumulate(): rows * (weights_blk * resid)  13.6 us
    dot_general x16, matrix products, accumulate(): jnp.dot(stacked, one_hot, precision=lax.Precision.HIGHEST, preferred_elem...  13.1 us
    mul x16, other arithmetic, accumulate(): weights_blk * resid  11.1 us
  transfers between devices with their start and end apart: 1, of which 1 were waited for; matrix products, arithmetic and copies ran while one was open for 0% of the time, Pallas kernels for 0%

commit v1 on v0

--- a/solution.py
+++ b/solution.py
@@ -88,7 +88,9 @@
     solution_own = block_solve(make_reader(own_part), own_part[pair_count:], damping)
     unit_terms = quadratic_terms(make_reader(own_part), own_part[pair_count:], solution_own)
     before = jnp.sum(weights_on * residual * residual)
-    chi_total, weight_total = lax.psum((before + unit_terms, jnp.sum(weights_on)), ("tm", "src"))
+    chi_total, weight_total = lax.psum(
+        lax.psum((before + unit_terms, jnp.sum(weights_on)), "tm"), "src"
+    )
     return (solution_own, chi_total / weight_total)
 
 

time: 244 us -> 239 us (0.980)
  blocking collectives: 41.3 us -> 36.7 us
    psum x1 -> x2, blocking collectives: 41.3 us -> 36.7 us  [the longest x1 31.2 us: on_device(): lax.psum(lax.psum((before + unit_terms, jnp.sum(weights_on)), 'tm'), 'src')]
where the time goes in v1:
time: 239 us; the launch traced here: 236 us
  waiting for transfers between devices  90.6 us (38%)
  other arithmetic  62.9 us (26%)
  blocking collectives  36.7 us (15%)
  between operations  30 us (13%)
  matrix products  13.1 us (5%)
    unnamed x2, waiting for transfers between devices  90.6 us
    psum x1, blocking collectives, on_device(): lax.psum(lax.psum((before + unit_terms, jnp.sum(weights_on)), 'tm'), 'src')  31.2 us
    reduce_sum x16, other arithmetic, quadratic_terms(): quadratic = quadratic + jnp.sum(solution_own[i] * applied)  24 us
    mul x16, other arithmetic, accumulate(): rows * (weights_blk * resid)  13.6 us
    dot_general x16, matrix products, accumulate(): jnp.dot(stacked, one_hot, precision=lax.Precision.HIGHEST, preferred_elem...  13.1 us
    mul x16, other arithmetic, accumulate(): weights_blk * resid  11.1 us
    psum x1, blocking collectives, on_device(): lax.psum((before + unit_terms, jnp.sum(weights_on)), 'tm')  5.52 us
  transfers between devices with their start and end apart: 1, of which 1 were waited for; matrix products, arithmetic and copies ran while one was open for 0% of the time, Pallas kernels for 0%

profile of v1, /device:TPU:0, one launch (start us, length us, event | category | flops | bytes accessed | tf_op | source)
XLA Modules:
  0.0 236.4 jit_solution(5982645079641946937)
XLA Ops:
  8.7 1.6 fusion.56
  10.3 42.7 %while.14 = (s32[]{:T(128)}, f32[272,128]{1,0:T(8,128)S(1)}, f32[16,16384]{1,0:T(8,128)}, f32[16384]{0:T(1024)S(1)}, f32[16384]{0:T(1024)}, /*index=5*/s32[16384...) while((s32[]{:T(128)}, f32[272,128]{1,0:T(8,128)S(1)}, f32[16,16384]{1,0:T(8,128)}, ...), condition=%wide.region_1.2_spmd.clone, body=%wide.region_0.1_spmd.clone.sunk | while | flops 428839936 | bytes 4837545 | solution.py:86
  11.0 0.8 broadcast_multiply_fusion.4
  13.7 0.8 broadcast_multiply_fusion.4
  16.3 0.8 broadcast_multiply_fusion.4
  19.0 0.8 broadcast_multiply_fusion.4
  24.4 0.8 broadcast_multiply_fusion.4
  27.0 0.8 broadcast_multiply_fusion.4
  54.9 90.6 %all-reduce.5.cloned.1.call-done = f32[272,128]{1,0:T(8,128)} async-done(((f32[272,128]{1,0:T(8,128)}), f32[272,128]{1,0:T(8,128)}) %all-reduce.5.cloned.1.call-update) | async-done | bytes 139280
  145.5 1.0 subtract_divide_fusion.110
  146.4 1.2 subtract_sqrt_fusion.8
  147.7 2.8 %subtract_divide_fusion.29 = (f32[8]{0:T(128)S(1)}, f32[8]{0:T(128)S(1)}, f32[8]{0:T(128)S(1)}, f32[8]{0:T(128)S(1)}, f32[8]{0:T(128)S(1)}, /*index=5*/f32[8]{0:...) fusion(f32[272,128]{1,0:T(8,128)} %all-reduce.5.cloned.1.call-d, ...), kind=kLoop, calls=%fused_computation.264 | loop fusion | flops 10472 | bytes 10624 | tf_op jit(solution)/shard_map/div | solution.py:33
  150.5 1.5 subtract_divide_fusion.15
  152.0 1.9 multiply_reduce_fusion
  154.6 1.4 fusion.9
  156.8 1.5 multiply_reduce_fusion.14
  158.2 1.4 multiply_reduce_fusion.15
  161.0 1.5 multiply_reduce_fusion.13
  163.2 1.5 multiply_reduce_fusion.12
  165.3 1.5 multiply_reduce_fusion.11
  167.5 1.5 multiply_reduce_fusion.10
  169.7 1.5 multiply_reduce_fusion.9
  171.8 1.5 multiply_reduce_fusion.8
  174.0 1.5 multiply_reduce_fusion.7
  176.2 1.5 multiply_reduce_fusion.6
  178.3 1.5 multiply_reduce_fusion.5
  180.5 1.5 multiply_reduce_fusion.4
  182.7 1.5 multiply_reduce_fusion.3
  184.8 1.5 multiply_reduce_fusion.2
  187.0 1.5 multiply_reduce_fusion.1
  190.5 5.5 %all-reduce.2 = (f32[]{:T(128)}, f32[]{:T(128)}) all-reduce(f32[]{:T(128)S(6)} %add.1130, f32[]{:T(128)} %get-tuple-element.154), channel_id=1, replica_groups=mesh['tm'=2,'src'=16] {'tm'}, use_global_device_ids=true, to_apply=%region_21.22 | all-reduce | flops 2 | bytes 16 | tf_op jit(solution)/shard_map/psum | solution.py:92
  196.0 31.2 %all-reduce.1 = (f32[]{:T(128)}, f32[]{:T(128)}) all-reduce(f32[]{:T(128)} %get-tuple-element.170, f32[]{:T(128)} %get-tuple-element.171), channel_id=1, replica_groups=mesh['tm'=2,'src'=16] {'src'}, use_global_device_ids=true, to_apply=%region_22.23 | all-reduce | flops 2 | bytes 16 | tf_op jit(solution)/shard_map/psum | solution.py:91
  (103 shorter events, 39.5 us)
Async XLA Ops:
  7.2 138.3 %all-reduce.5.cloned.1.call-start = ((), (), s32[]{:S(2)}) async-start(), calls=%async_computation | async-start | bytes 278528
  10.3 43.4 %copy-start.2 = (u32[32]{0:T(128)S(1)}, u32[32]{0:T(128)}, u32[]{:S(2)}) copy-start(u32[32]{0:T(128)} %constant.48) | copy-start | bytes 388
  10.3 135.2 %copy-start.1 = (f32[8]{0:T(128)S(1)}, f32[8]{0:T(128)}, u32[]{:S(2)}) copy-start(f32[8]{0:T(128)} %param.13) | copy-start | bytes 100
  53.0 0.7 copy-start
Sparse Core Ops, SparseCore 0:
  53.8 91.6 all-reduce.4
